TPU v7x, 32 devices: a whole 2x2x4 slice. The times are simulated.
32 devices in a mesh: samples: 8 (over z, y), variants: 4 (over x, core).
Axes of the slice: x: 2, y: 2, z: 4, core: 2. Of those that a mesh axis runs over, the one named last changes fastest.
Arguments:
- genotypes: int32 [2048, 32768], P('variants', 'samples'), may hold values from 0 to 3, as said below
- weights: float32 [32768], P('samples'), may hold values from 0.25 to 20
Outputs:
- call_mean: float32 [2048], P('variants')
- call_var: float32 [2048], P('variants')
- class_counts: int32 [4, 2048], P(None, 'variants')
- ld_window: float32 [1024, 2048], P('samples', 'variants')
- sample_calls: int32 [2, 32768], P(None, 'samples')
- sample_share: float32 [32768], P('samples')
Inputs may be any that keep to these rules, and one draw needn't show every extreme that they name: `genotypes`: in every variant's row, each aligned group of 8 samples (samples 8 i to 8 i + 7) holds at least one call other than 3.
All inputs are finite; a program needn't handle non-finite values.
Results may differ from a plain program's by a relative error of at most 0.0004.
Values may be sent and summed in bfloat16 or wider, within the bound.
A program may use at most 64 MiB of HBM per device.

v0:
```python
import jax
import jax.numpy as jnp
from jax import lax
from jax.sharding import PartitionSpec as P


def shifted(value, axis, by):
    size = lax.axis_size(axis)
    pairs = [(i, i + by) for i in range(size) if 0 <= i + by < size]
    return lax.ppermute(value, axis, pairs)


def on_device(genotypes, weights):
    present = genotypes != 3
    called = present.astype(jnp.float32)
    dosage = jnp.where(present, genotypes, 0).astype(jnp.float32)
    weighted = called * weights[None, :]
    w_sum_part = jnp.sum(weighted, axis=1)
    first_part = jnp.sum(weighted * dosage, axis=1)
    classes = jnp.stack(
        [jnp.sum((genotypes == level).astype(jnp.float32), axis=1) for level in range(4)]
    )
    second_part = jnp.sum(weighted * dosage * dosage, axis=1)
    w_sum, first_total, second_total, class_total = lax.psum(
        (w_sum_part, first_part, second_part, classes), "samples"
    )
    mean_value = first_total / w_sum
    deviation = second_total - first_total * mean_value
    var_value = deviation / w_sum
    factor = 1.0 / jnp.sqrt(w_sum * (var_value + 1e-05))
    centered = (dosage - mean_value[:, None]) * called
    scaled = (jnp.sqrt(weights)[None, :] * centered * factor[:, None]).astype(jnp.bfloat16)
    following = shifted(scaled, "variants", -1)
    joined = jnp.concatenate([scaled, following], axis=0)
    rows_owned = joined.shape[0] // lax.axis_size("samples")
    partial_all = lax.dot_general(
        joined, scaled, (((1,), (1,)), ((), ())), preferred_element_type=jnp.float32
    )
    summed = lax.psum(partial_all, "samples")
    ld_window = lax.dynamic_slice_in_dim(
        summed, lax.axis_index("samples") * rows_owned, rows_owned, 0
    )
    squares = scaled.astype(jnp.float32)
    called_total, het_total, square_total = lax.psum(
        (
            jnp.sum(called, axis=0),
            jnp.sum((genotypes == 1).astype(jnp.float32), axis=0),
            jnp.sum(squares * squares, axis=0),
        ),
        "variants",
    )
    samples_all = weights.shape[0] * lax.axis_size("samples")
    variants_all = genotypes.shape[0] * lax.axis_size("variants")
    sample_share = square_total * (samples_all / variants_all)
    sample_calls = jnp.stack([called_total, het_total]).astype(jnp.int32)
    return (
        mean_value,
        var_value,
        class_total.astype(jnp.int32),
        ld_window,
        sample_calls,
        sample_share,
    )


def solution(mesh):
    placed = (P("variants", "samples"), P("samples"))
    return jax.shard_map(
        on_device,
        mesh=mesh,
        in_specs=placed,
        out_specs=(
            P("variants"),
            P("variants"),
            P(None, "variants"),
            P("samples", "variants"),
            P(None, "samples"),
            P("samples"),
        ),
        check_vma=False,
    )
```

profile of v0, /device:TPU:21, one launch (start us, length us, event | category | flops | bytes accessed | tf_op | source)
XLA Modules:
  0.0 223.7 jit_solution(9397429142286188237)
XLA Ops:
  7.2 0.0 copy-start.1
  7.2 0.0 all-reduce.4.cloned.1.call-start
  7.2 0.0 copy-start
  7.2 5.0 %convert_reduce_fusion = (f32[4096]{0:T(1024)S(1)}, f32[512]{0:T(512)S(1)}) fusion(s32[512,4096]{1,0:T(8,128)} %param.2), kind=kLoop, calls=%fused_computation | loop fusion | flops 8384000 | bytes 8407040 | tf_op jit(solution)/shard_map/reduce_sum | solution.py:47
  12.3 0.0 copy-done.1
  12.3 0.7 copy-done
  13.0 6.3 %fusion.2 = (f32[512]{0:T(512)S(1)}, f32[512]{0:T(512)S(1)}, f32[512]{0:T(512)S(1)}, f32[4096]{0:T(1024)S(1)}, f32[512]{0:T(512)S(1)}, /*index=5*/f32[512]{0:T(512)S(1)}, f32[512]{0:T(512)S(1)}) fusion(s32[512,4096]{1,0:T(8,128)S(1)} %copy-done, f32[4096]{0:T(1024)S(1)} %copy-done.1), kind=kLoop, calls=%fused_computation.6 | loop fusion | flops 41935872 | bytes 8433664 | tf_op jit(solution)/shard_map/reduce_sum | solution.py:23
  19.4 24.1 %all-reduce = (f32[512]{0:T(512)S(1)}, f32[512]{0:T(512)S(1)}, f32[512]{0:T(512)S(1)}, f32[4,512]{1,0:T(4,128)S(1)}) all-reduce(f32[512]{0:T(512)S(1)} %get-tuple-element.8, f32[512]{0:T(512)S(1)} %get-tuple-element.7, f32[512]{0:T(512)S(1)} %get-tuple-element.6, ...), channel_id=1, replica_groups=mesh['samples'=8,'variants'=4] {'samples'}, use_global_device_ids=true, to_apply=%region_1.2 | all-reduce | flops 3584 | bytes 28672 | tf_op jit(solution)/shard_map/psum | solution.py:24
  43.4 0.6 multiply_rsqrt_fusion
  44.0 0.0 copy-start.2
  44.0 5.2 %multiply_reduce_fusion = (f32[4096]{0:T(1024)S(1)}, bf16[512,4096]{1,0:T(8,128)(2,1)S(1)}) fusion(f32[512]{0:T(512)S(1)} %get-tuple-element.24, f32[512]{0:T(512)S(1)} %get-tuple-element.26, s32[512,4096]{1,0:T(8,128)} %param.2, f32[4096]{0:T(1024)S(1)} %sqrt.6), kind=kLoop, calls=%fused_computation.11 | loop fusion | flops 23064576 | bytes 12619776 | tf_op jit(solution)/shard_map/reduce_sum | solution.py:48
  49.2 9.4 %collective-permute-start = (bf16[512,4096]{1,0:T(8,128)(2,1)S(1)}, bf16[512,4096]{1,0:T(8,128)(2,1)S(1)}, u32[]{:S(2)}, u32[]{:S(2)}) collective-permute-start(bf16[512,4096]{1,0:T(8,128)(2,1)S(1)} %get-tuple-element.23), channel_id=1, source_target_pairs={{1,0},{2,1},{3,2},{5,4},{6,5},{7,6},{9,8},{10,9},{11,10},{13,12},{... | collective-permute-start | bytes 12582920 | tf_op jit(solution)/shard_map/ppermute | solution.py:10
  58.6 47.3 %collective-permute-done = bf16[512,4096]{1,0:T(8,128)(2,1)S(1)} collective-permute-done((bf16[512,4096]{1,0:T(8,128)(2,1)S(1)}, bf16[512,4096]{1,0:T(8,128)(2,1)S(1)}, u32[]{:S(2)}, u32[]{:S(2)}) %collective-permute-start) | collective-permute-done | bytes 4194336 | tf_op jit(solution)/shard_map/ppermute | solution.py:10
  105.9 5.8 %fusion.3 = f32[1024,512]{1,0:T(8,128)} fusion(bf16[512,4096]{1,0:T(8,128)(2,1)S(1)} %get-tuple-element.23, bf16[512,4096]{1,0:T(8,128)(2,1)S(1)} %collective-permute-done), kind=kOutput, calls=%fused_computation.7 | convolution fusion | flops 4311744512 | bytes 10485760 | tf_op jit(solution)/shard_map/dot_general | solution.py:36
  111.7 0.0 copy-done.2
  111.7 0.0 all-reduce.4.cloned.1.call-update
  111.7 0.6 convert_element_type.36
  112.3 10.8 %all-reduce.1 = (f32[1,4096]{1,0:T(1,128)S(1)}, f32[1,4096]{1,0:T(1,128)S(1)}, f32[4096]{0:T(1024)S(1)}) all-reduce(f32[1,4096]{1,0:T(1,128)S(1)} %bitcast.7, f32[1,4096]{1,0:T(1,128)S(1)} %bitcast.8, f32[4096]{0:T(1024)S(1)} %get-tuple-element.22), channel_id=1, replica_groups=mesh['samples'=8,'variants'=4] {'variants'}, use_global_device_ids=true, to_apply=%region_15.16 | all-reduce | flops 12288 | bytes 98304 | tf_op jit(solution)/shard_map/psum | solution.py:44
  123.2 0.6 broadcast_multiply_fusion
  123.8 0.7 maximum_convert_fusion
  124.4 90.7 %all-reduce.4.cloned.1.call-done = f32[1024,512]{1,0:T(8,128)} async-done(((f32[1024,512]{1,0:T(8,128)}), f32[1024,512]{1,0:T(8,128)}) %all-reduce.4.cloned.1.call-update) | async-done | bytes 2097168 | tf_op jit(solution)/shard_map/psum | solution.py:39
  215.2 1.7 constant_dynamic-slice_fusion
  (2 shorter events, 0.0 us)
Async XLA Ops:
  7.2 5.1 %copy-start.1 = (f32[4096]{0:T(1024)S(1)}, f32[4096]{0:T(1024)}, u32[]{:S(2)}) copy-start(f32[4096]{0:T(1024)} %param.3) | copy-start | bytes 49156
  7.2 208.0 %all-reduce.4.cloned.1.call-start = ((), (), s32[]{:S(2)}) async-start(), calls=%async_computation | async-start | bytes 4194304 | tf_op jit(solution)/shard_map/psum | solution.py:39
  7.2 5.8 %copy-start = (s32[512,4096]{1,0:T(8,128)S(1)}, s32[512,4096]{1,0:T(8,128)}, u32[]{:S(2)}) copy-start(s32[512,4096]{1,0:T(8,128)} %param.2) | copy-start | bytes 25165828
  44.0 67.7 %copy-start.2 = (f32[512]{0:T(512)}, f32[512]{0:T(512)S(1)}, u32[]{:S(2)}) copy-start(f32[512]{0:T(512)S(1)} %get-tuple-element.26) | copy-start | bytes 6148
  49.2 56.7 %collective-permute-start = (bf16[512,4096]{1,0:T(8,128)(2,1)S(1)}, bf16[512,4096]{1,0:T(8,128)(2,1)S(1)}, u32[]{:S(2)}, u32[]{:S(2)}) collective-permute-start(bf16[512,4096]{1,0:T(8,128)(2,1)S(1)} %get-tuple-element.23), channel_id=1, source_target_pairs={{1,0},{2,1},{3,2},{5,4},{6,5},{7,6},{9,8},{10,9},{11,10},{13,12},{... | collective-permute-start | bytes 12582920 | tf_op jit(solution)/shard_map/ppermute | solution.py:10
Sparse Core Ops, SparseCore 0:
  111.9 103.2 all-reduce.3
where the time goes:
time: 227 us; the launch traced here: 224 us
  waiting for transfers between devices  138 us (61%)
  blocking collectives  34.9 us (15%)
  other arithmetic  19 us (8%)
  between operations  14.1 us (6%)
  starting transfers between devices  9.46 us (4%)
  matrix products  5.81 us (3%)
  local copies, waits for them, and re-layouts  2.4 us (1%)
    psum x1, waiting for transfers between devices, on_device(): summed = lax.psum(partial_all, 'samples')  90.7 us
    ppermute x1, waiting for transfers between devices, shifted(): return lax.ppermute(value, axis, pairs)  47.3 us
    psum x1, blocking collectives, on_device(): lax.psum((w_sum_part, first_part, second_part, classes), 'samples')  24.1 us
    psum x1, blocking collectives, on_device(): lax.psum((jnp.sum(called, axis=0), jnp.sum((genotypes == 1).astype(jnp.fl...  10.8 us
    ppermute x1, starting transfers between devices, shifted(): return lax.ppermute(value, axis, pairs)  9.42 us
    reduce_sum x1, other arithmetic, on_device(): second_part = jnp.sum(weighted * dosage * dosage, axis=1)  6.32 us
    dot_general x1, matrix products, on_device(): lax.dot_general(joined, scaled, (((1,), (1,)), ((), ())), preferred_eleme...  5.81 us
    reduce_sum x1, other arithmetic, on_device(): jnp.sum(squares * squares, axis=0)  5.17 us
  transfers between devices with their start and end apart: 2, of which 2 were waited for; matrix products, arithmetic and copies ran while one was open for 1% of the time, Pallas kernels for 0%

commit v1 on v0

v1 whole, which is shorter than its diff:
```python
import functools

import jax
import jax.numpy as jnp
from jax import lax
from jax.experimental import pallas as pl
from jax.experimental.pallas import tpu as pltpu
from jax.sharding import PartitionSpec as P

MESH = pl.DeviceIdType.MESH
F32 = jnp.float32
BF16 = jnp.bfloat16
LANES = 128
STEP = 16
SLAB = 512


def kernel(
    S,
    V,
    CH,
    gen_hbm,
    w_ref,
    stat_out,
    count_out,
    ld_out,
    call_out,
    share_out,
    gen,
    code,
    ncode,
    scaled,
    nscaled,
    part,
    rcv,
    wacc,
    cacc,
    sacc,
    qacc,
    root,
    gat,
    par,
    npar,
    colm,
    colf,
    smp,
    gen_sem,
    code_send,
    code_recv,
    stat_send,
    stat_recv,
    par_send,
    par_recv,
    rs_send,
    rs_recv,
    smp_send,
    smp_recv,
):
    s = lax.axis_index("samples")
    v = lax.axis_index("variants")
    rows, width = gen.shape
    R = 2 * rows // S
    H = S // 2
    NC = rows // CH
    blocks = width // LANES
    slabs = width // SLAB
    has_next = v < V - 1
    has_prev = v > 0

    def chunk_rows(c):
        return pl.ds(pl.multiple_of(c * CH, CH), CH)

    def load(k):
        c = lax.rem(k + s, NC)
        return pltpu.make_async_copy(
            gen_hbm.at[chunk_rows(c)], gen.at[chunk_rows(c)], gen_sem.at[c]
        )

    def start_load(k, _):
        load(k).start()
        return 0

    lax.fori_loop(0, NC, start_load, 0)

    barrier = pltpu.get_barrier_semaphore()

    def greet_samples(d, _):
        pl.semaphore_signal(
            barrier,
            inc=1,
            device_id={"samples": lax.rem(s + d, S)},
            device_id_type=MESH,
        )
        return 0

    def greet_variants(d, _):
        pl.semaphore_signal(
            barrier,
            inc=1,
            device_id={"variants": lax.rem(v + d, V)},
            device_id_type=MESH,
        )
        return 0

    lax.fori_loop(1, S, greet_samples, 0)
    lax.fori_loop(1, V, greet_variants, 0)

    root[...] = jnp.sqrt(w_ref[...])
    sacc[...] = jnp.zeros_like(sacc)
    qacc[...] = jnp.zeros_like(qacc)

    def code_copy(c):
        return pltpu.make_async_remote_copy(
            src_ref=code.at[chunk_rows(c)],
            dst_ref=ncode.at[chunk_rows(c)],
            send_sem=code_send.at[c],
            recv_sem=code_recv.at[c],
            device_id={"variants": lax.rem(v + V - 1, V)},
            device_id_type=MESH,
        )

    def first_pass(k, _):
        c = lax.rem(k + s, NC)
        load(k).wait()

        def sixteen(i, _):
            here = pl.ds(pl.multiple_of(c * CH + i * STEP, STEP), STEP)
            zero = jnp.zeros((STEP, LANES), F32)
            w0, w1, w2 = zero, zero, zero
            cnt = jnp.zeros((STEP, LANES), jnp.int32)
            for b in range(blocks):
                lane = slice(b * LANES, (b + 1) * LANES)
                g = gen[here, lane]
                w = jnp.broadcast_to(w_ref[0:1, lane], (STEP, LANES))
                w0 = w0 + jnp.where(g == 0, w, 0.0)
                w1 = w1 + jnp.where(g == 1, w, 0.0)
                w2 = w2 + jnp.where(g == 2, w, 0.0)
                tag = jnp.left_shift(jnp.int32(1), jnp.left_shift(g, 3))
                cnt = cnt + tag
                sacc[:, lane] += tag[:8] + tag[8:]
                code[here, lane] = g.astype(F32).astype(BF16)
            wacc[0, here] = w0
            wacc[1, here] = w1
            wacc[2, here] = w2
            cacc[here] = cnt
            return 0

        lax.fori_loop(0, CH // STEP, sixteen, 0)

        @pl.when(k == 0)
        def _():
            pl.semaphore_wait(barrier, S + V - 2)

        @pl.when(has_prev)
        def _():
            code_copy(c).start()

        return 0

    lax.fori_loop(0, NC, first_pass, 0)

    def total(x):
        return jnp.sum(x.T, axis=0, keepdims=True)

    cnt = cacc[...]
    lines = [total(wacc[i]) for i in range(3)]
    for level in range(4):
        lines.append(
            total(jnp.bitwise_and(jnp.right_shift(cnt, 8 * level), 255).astype(F32))
        )
    lines.append(jnp.zeros_like(lines[0]))
    gat[s] = jnp.concatenate(lines, axis=0)

    def stat_copy(d, slot):
        return pltpu.make_async_remote_copy(
            src_ref=gat.at[slot],
            dst_ref=gat.at[slot],
            send_sem=stat_send.at[d],
            recv_sem=stat_recv.at[slot],
            device_id={"samples": lax.rem(s + d, S)},
            device_id_type=MESH,
        )

    def send_stat(d, _):
        stat_copy(d, s).start()
        return 0

    lax.fori_loop(1, S, send_stat, 0)

    def wait_stat(d, _):
        stat_copy(d, lax.rem(s + d, S)).wait_recv()
        return 0

    lax.fori_loop(1, S, wait_stat, 0)
    sums = gat[0]
    for t in range(1, S):
        sums = sums + gat[t]
    w0, w1, w2 = sums[0:1], sums[1:2], sums[2:3]
    w_sum = w0 + w1 + w2
    mean = (w1 + 2.0 * w2) / w_sum
    one, two = 1.0 - mean, 2.0 - mean
    var = (w0 * mean * mean + w1 * one * one + w2 * two * two) / w_sum
    factor = 1.0 / jnp.sqrt(w_sum * (var + 1e-05))
    stat_out[...] = jnp.concatenate([mean, var], axis=0)
    count_out[...] = sums[3:7].astype(jnp.int32)
    par[...] = jnp.concatenate([mean, factor, jnp.zeros((6, rows), F32)], axis=0)

    par_copy = pltpu.make_async_remote_copy(
        src_ref=par,
        dst_ref=npar,
        send_sem=par_send.at[0],
        recv_sem=par_recv.at[0],
        device_id={"variants": lax.rem(v + V - 1, V)},
        device_id_type=MESH,
    )

    @pl.when(has_prev)
    def _():
        par_copy.start()

    def columns(ref):
        turned = ref[...].T
        colm[...] = jnp.broadcast_to(turned[:, 0:1], colm.shape)
        colf[...] = jnp.broadcast_to(turned[:, 1:2], colf.shape)

    def scale(src, src_row, dst, dst_row, count, squares):
        def sixteen(i, _):
            here = pl.ds(pl.multiple_of(src_row + i * STEP, STEP), STEP)
            there = pl.ds(pl.multiple_of(dst_row + i * STEP, STEP), STEP)
            m, f = colm[here], colf[here]
            for b in range(blocks):
                lane = slice(b * LANES, (b + 1) * LANES)
                d = src[here, lane].astype(F32)
                r = jnp.broadcast_to(root[0:1, lane], (STEP, LANES))
                x = jnp.where(d < 2.5, r * (d - m) * f, 0.0).astype(BF16)
                dst[there, lane] = x
                if squares:
                    y = x.astype(F32)
                    y = y * y
                    qacc[:, lane] += y[:8] + y[8:]
            return 0

        lax.fori_loop(0, count // STEP, sixteen, 0)

    columns(par)
    scale(code, 0, scaled, 0, rows, True)

    def rs_copy(owner, slot):
        return pltpu.make_async_remote_copy(
            src_ref=part.at[owner],
            dst_ref=rcv.at[slot],
            send_sem=rs_send.at[owner],
            recv_sem=rs_recv.at[slot],
            device_id={"samples": owner},
            device_id_type=MESH,
        )

    def correlate(left):
        return lax.dot_general(
            left, scaled[...], (((1,), (1,)), ((), ())), preferred_element_type=F32
        )

    def own_rows(k, _):
        owner = lax.rem(s + k, H)
        rows_here = pl.ds(pl.multiple_of(owner * R, R), R)
        part[owner] = correlate(scaled[rows_here, :])

        @pl.when(owner != s)
        def _():
            rs_copy(owner, s).start()

        return 0

    lax.fori_loop(0, H, own_rows, 0)

    packed = sacc[...]
    tags = [
        jnp.bitwise_and(jnp.right_shift(packed, 8 * level), 255).astype(F32)
        for level in range(3)
    ]
    for q, value in enumerate([tags[0] + tags[1] + tags[2], tags[1], qacc[...]]):
        line = jnp.sum(value, axis=0, keepdims=True)
        for i in range(slabs):
            smp[v, pl.ds(q * slabs + i, 1), :] = line[:, i * SLAB : (i + 1) * SLAB]

    def smp_copy(d, slot):
        return pltpu.make_async_remote_copy(
            src_ref=smp.at[slot],
            dst_ref=smp.at[slot],
            send_sem=smp_send.at[d],
            recv_sem=smp_recv.at[slot],
            device_id={"variants": lax.rem(v + d, V)},
            device_id_type=MESH,
        )

    def send_smp(d, _):
        smp_copy(d, v).start()
        return 0

    lax.fori_loop(1, V, send_smp, 0)

    @pl.when(has_next)
    def _():
        par_copy.wait_recv()
        columns(npar)

        def cross(k, _):
            c = lax.rem(k + s, NC)
            code_copy(c).wait_recv()
            scale(ncode, c * CH, nscaled, 0, CH, False)
            got = correlate(nscaled[...])
            for i in range(CH // R):
                owner = H + c * (CH // R) + i
                part[owner] = got[i * R : (i + 1) * R]

                @pl.when(owner != s)
                def _():
                    rs_copy(owner, s).start()

            return 0

        lax.fori_loop(0, NC, cross, 0)

    def wait_smp(d, _):
        smp_copy(d, lax.rem(v + d, V)).wait_recv()
        return 0

    lax.fori_loop(1, V, wait_smp, 0)
    all_sums = smp[0]
    for t in range(1, V):
        all_sums = all_sums + smp[t]
    call_out[...] = all_sums[: 2 * slabs].astype(jnp.int32)
    share_out[...] = all_sums[2 * slabs :] * F32((width * S) / (rows * V))

    sent_to_me = jnp.logical_or(s < H, has_next)

    @pl.when(sent_to_me)
    def _():
        ld_out[...] = part[s]

        def gather(d, _):
            t = lax.rem(s + d, S)
            rs_copy(s, t).wait_recv()
            ld_out[...] += rcv[t]
            return 0

        lax.fori_loop(1, S, gather, 0)

    @pl.when(jnp.logical_not(sent_to_me))
    def _():
        ld_out[...] = jnp.zeros_like(ld_out)

    def drain_samples(d, _):
        stat_copy(d, s).wait_send()
        owner = lax.rem(s + d, S)

        @pl.when(jnp.logical_or(owner < H, has_next))
        def _():
            rs_copy(owner, s).wait_send()

        return 0

    lax.fori_loop(1, S, drain_samples, 0)

    def drain_variants(d, _):
        smp_copy(d, v).wait_send()
        return 0

    lax.fori_loop(1, V, drain_variants, 0)

    @pl.when(has_prev)
    def _():
        par_copy.wait_send()

        def drain_codes(c, _):
            code_copy(c).wait_send()
            return 0

        lax.fori_loop(0, NC, drain_codes, 0)


def on_device(S, V, genotypes, weights):
    rows, width = genotypes.shape
    R = 2 * rows // S
    CH = max(128, R)
    NC = rows // CH
    slabs = width // SLAB
    vmem = pl.BlockSpec(memory_space=pltpu.VMEM)
    dma = pltpu.SemaphoreType.DMA
    stats, counts, ld, calls, share = pl.pallas_call(
        functools.partial(kernel, S, V, CH),
        out_shape=(
            jax.ShapeDtypeStruct((2, rows), F32),
            jax.ShapeDtypeStruct((4, rows), jnp.int32),
            jax.ShapeDtypeStruct((R, rows), F32),
            jax.ShapeDtypeStruct((2 * slabs, SLAB), jnp.int32),
            jax.ShapeDtypeStruct((slabs, SLAB), F32),
        ),
        in_specs=[pl.BlockSpec(memory_space=pl.ANY), vmem],
        out_specs=(vmem,) * 5,
        scratch_shapes=[
            pltpu.VMEM((rows, width), jnp.int32),
            pltpu.VMEM((rows, width), BF16),
            pltpu.VMEM((rows, width), BF16),
            pltpu.VMEM((rows, width), BF16),
            pltpu.VMEM((CH, width), BF16),
            pltpu.VMEM((S, R, rows), F32),
            pltpu.VMEM((S, R, rows), F32),
            pltpu.VMEM((3, rows, LANES), F32),
            pltpu.VMEM((rows, LANES), jnp.int32),
            pltpu.VMEM((8, width), jnp.int32),
            pltpu.VMEM((8, width), F32),
            pltpu.VMEM((1, width), F32),
            pltpu.VMEM((S, 8, rows), F32),
            pltpu.VMEM((8, rows), F32),
            pltpu.VMEM((8, rows), F32),
            pltpu.VMEM((rows, LANES), F32),
            pltpu.VMEM((rows, LANES), F32),
            pltpu.VMEM((V, 3 * slabs, SLAB), F32),
            dma((NC,)),
            dma((NC,)),
            dma((NC,)),
            dma((S,)),
            dma((S,)),
            dma((1,)),
            dma((1,)),
            dma((S,)),
            dma((S,)),
            dma((V,)),
            dma((V,)),
        ],
        compiler_params=pltpu.CompilerParams(
            collective_id=0, has_side_effects=True, vmem_limit_bytes=60 * 1024 * 1024
        ),
        name="window_stats",
    )(genotypes, weights.reshape(1, width))
    return (
        stats[0],
        stats[1],
        counts,
        ld,
        calls.reshape(2, width),
        share.reshape(width),
    )


def solution(mesh):
    body = functools.partial(on_device, mesh.shape["samples"], mesh.shape["variants"])
    return jax.shard_map(
        body,
        mesh=mesh,
        in_specs=(P("variants", "samples"), P("samples")),
        out_specs=(
            P("variants"),
            P("variants"),
            P(None, "variants"),
            P("samples", "variants"),
            P(None, "samples"),
            P("samples"),
        ),
        check_vma=False,
    )
```

time: 227 us -> 89.2 us (0.39); the launches traced: 224 us -> 88.8 us
  waiting for transfers between devices: 138 us -> 0 us
  Pallas kernels: 0 us -> 81.1 us
  blocking collectives: 34.9 us -> 0 us
  other arithmetic: 19 us -> 0 us
  between operations: 14.1 us -> 0.64 us
  starting transfers between devices: 9.46 us -> 0 us
  matrix products: 5.81 us -> 0 us
  local copies, waits for them, and re-layouts: 2.4 us -> 7.03 us
    psum x1 -> x0, waiting for transfers between devices: 90.7 us -> none  [on_device(): summed = lax.psum(partial_all, 'samples')]
    pallas_call x0 -> x1, Pallas kernels: none -> 81.1 us  [on_device(): pl.pallas_call(functools.partial(kernel, S, V, CH), out_shape=(jax.ShapeD...]
    ppermute x1 -> x0, waiting for transfers between devices: 47.3 us -> none  [shifted(): return lax.ppermute(value, axis, pairs)]
    psum x2 -> x0, blocking collectives: 34.9 us -> none  [the longest x1 24.1 us: on_device(): lax.psum((w_sum_part, first_part, second_part, classes), 'samples')]
    reduce_sum x3 -> x0, other arithmetic: 16.5 us -> none  [the longest x1 6.32 us: on_device(): second_part = jnp.sum(weighted * dosage * dosage, axis=1)]
    ppermute x1 -> x0, starting transfers between devices: 9.42 us -> none  [shifted(): return lax.ppermute(value, axis, pairs)]
    dot_general x1 -> x0, matrix products: 5.81 us -> none  [on_device(): lax.dot_general(joined, scaled, (((1,), (1,)), ((), ())), preferred_eleme...]
    unnamed x6 -> x3, local copies, waits for them, and re-layouts: 0.72 us -> 4.29 us
  transfers between devices with their start and end apart: 2 -> 0, of which waited for: 2 -> 0; matrix products, arithmetic and copies ran while one was open for 1% -> 0% of each run, Pallas kernels for 0% -> 0%
where the time goes in v1:
time: 89.2 us; the launch traced here: 88.8 us
  Pallas kernels  81.1 us (91%)
  local copies, waits for them, and re-layouts  7.03 us (8%)
    pallas_call x1, Pallas kernels, on_device(): pl.pallas_call(functools.partial(kernel, S, V, CH), out_shape=(jax.ShapeD...  81.1 us
    unnamed x3, local copies, waits for them, and re-layouts  4.29 us

profile of v1, /device:TPU:21, one launch (start us, length us, event | category | flops | bytes accessed | tf_op | source)
XLA Modules:
  0.0 88.8 jit_solution(16234052351065368298)
XLA Ops:
  0.6 81.1 %window_stats.1 = (f32[2,512]{1,0:T(2,128)}, s32[4,512]{1,0:T(4,128)}, f32[128,512]{1,0:T(8,128)}, s32[16,512]{1,0:T(8,128)}, f32[8,512]{1,0:T(8,128)}) custom-call(s32[512,4096]{1,0:T(8,128)} %gen_hbm.1, f32[1,4096]{1,0:T(1,128)} %bitcast.5), custom_call_target="tpu_custom_call" | custom-call | tf_op jit(solution)/shard_map/window_stats/pallas_call | solution.py:390
  81.7 1.3 %fusion = (f32[1,512]{1,0:T(1,128)}, f32[1,512]{1,0:T(1,128)}) fusion(f32[2,512]{1,0:T(2,128)} %get-tuple-element.11), kind=kLoop, calls=%fused_computation | loop fusion | bytes 8192 | tf_op jit(solution)/shard_map/slice | solution.py:439
  83.1 1.3 %copy.8 = f32[1,4,8,128]{3,1,2,0:T(4,128)} copy(f32[1,4,8,128]{3,2,1,0:T(8,128)} %bitcast.7) | data formatting | bytes 32768
  84.4 1.4 %reshape.22 = s32[2,4096]{1,0:T(2,128)} reshape(s32[16,512]{1,0:T(8,128)} %get-tuple-element.14) | data formatting | bytes 65536 | tf_op jit(solution)/shard_map/reshape | solution.py:442
  85.8 1.3 %copy.11 = s32[4,512]{1,0:T(4,128)} copy(s32[4,512]{1,0:T(4,128)} %get-tuple-element.26) | data formatting | bytes 16384
  87.1 1.7 %copy.12 = f32[128,512]{1,0:T(8,128)} copy(f32[128,512]{1,0:T(8,128)} %get-tuple-element.27) | data formatting | bytes 524288

commit v2 on v1

--- a/solution.py
+++ b/solution.py
@@ -12,6 +12,8 @@
 BF16 = jnp.bfloat16
 LANES = 128
 STEP = 16
+SUB = 32
+FULL = 32400.0
 SLAB = 512
 
 
@@ -32,6 +34,7 @@
     scaled,
     nscaled,
     part,
+    mine,
     rcv,
     wacc,
     cacc,
@@ -39,10 +42,13 @@
     qacc,
     root,
     gat,
+    ngat,
     par,
-    npar,
     colm,
     colf,
+    cole,
+    tall,
+    ntall,
     smp,
     gen_sem,
     code_send,
@@ -119,6 +125,17 @@
             device_id_type=MESH,
         )
 
+    def piece_copy(c, h):
+        here = pl.ds(pl.multiple_of(c * CH + h * SUB, SUB), SUB)
+        return pltpu.make_async_remote_copy(
+            src_ref=code.at[here],
+            dst_ref=ncode.at[here],
+            send_sem=code_send.at[c],
+            recv_sem=code_recv.at[c],
+            device_id={"variants": lax.rem(v + V - 1, V)},
+            device_id_type=MESH,
+        )
+
     def first_pass(k, _):
         c = lax.rem(k + s, NC)
         load(k).wait()
@@ -145,16 +162,20 @@
             cacc[here] = cnt
             return 0
 
-        lax.fori_loop(0, CH // STEP, sixteen, 0)
-
-        @pl.when(k == 0)
-        def _():
-            pl.semaphore_wait(barrier, S + V - 2)
-
-        @pl.when(has_prev)
-        def _():
-            code_copy(c).start()
-
+        def piece(h, _):
+            lax.fori_loop(h * (SUB // STEP), (h + 1) * (SUB // STEP), sixteen, 0)
+
+            @pl.when(jnp.logical_and(k == 0, h == 0))
+            def _():
+                pl.semaphore_wait(barrier, S + V - 2)
+
+            @pl.when(has_prev)
+            def _():
+                piece_copy(c, h).start()
+
+            return 0
+
+        lax.fori_loop(0, CH // SUB, piece, 0)
         return 0
 
     lax.fori_loop(0, NC, first_pass, 0)
@@ -192,22 +213,28 @@
         return 0
 
     lax.fori_loop(1, S, wait_stat, 0)
-    sums = gat[0]
-    for t in range(1, S):
-        sums = sums + gat[t]
-    w0, w1, w2 = sums[0:1], sums[1:2], sums[2:3]
-    w_sum = w0 + w1 + w2
-    mean = (w1 + 2.0 * w2) / w_sum
-    one, two = 1.0 - mean, 2.0 - mean
-    var = (w0 * mean * mean + w1 * one * one + w2 * two * two) / w_sum
-    factor = 1.0 / jnp.sqrt(w_sum * (var + 1e-05))
-    stat_out[...] = jnp.concatenate([mean, var], axis=0)
-    count_out[...] = sums[3:7].astype(jnp.int32)
-    par[...] = jnp.concatenate([mean, factor, jnp.zeros((6, rows), F32)], axis=0)
+
+    def moments(ref):
+        sums = ref[0]
+        for t in range(1, S):
+            sums = sums + ref[t]
+        w0, w1, w2 = sums[0:1], sums[1:2], sums[2:3]
+        w_sum = w0 + w1 + w2
+        mean = (w1 + 2.0 * w2) / w_sum
+        one, two = 1.0 - mean, 2.0 - mean
+        var = (w0 * mean * mean + w1 * one * one + w2 * two * two) / w_sum
+        factor = 1.0 / jnp.sqrt(w_sum * (var + 1e-05))
+        return sums, mean, var, factor
+
+    def norm(ref, t, mean, factor):
+        w0, w1, w2 = ref[t, 0:1], ref[t, 1:2], ref[t, 2:3]
+        one, two = 1.0 - mean, 2.0 - mean
+        length = jnp.sqrt(w0 * mean * mean + w1 * one * one + w2 * two * two)
+        return jnp.maximum(length * factor, 1e-12)
 
     par_copy = pltpu.make_async_remote_copy(
-        src_ref=par,
-        dst_ref=npar,
+        src_ref=gat,
+        dst_ref=ngat,
         send_sem=par_send.at[0],
         recv_sem=par_recv.at[0],
         device_id={"variants": lax.rem(v + V - 1, V)},
@@ -218,10 +245,22 @@
     def _():
         par_copy.start()
 
-    def columns(ref):
-        turned = ref[...].T
+    sums, mean, var, factor = moments(gat)
+    stat_out[...] = jnp.concatenate([mean, var], axis=0)
+    count_out[...] = sums[3:7].astype(jnp.int32)
+    level = FULL / norm(gat, s, mean, factor)
+
+    def columns(ref, mean, factor, turned_norms):
+        mine_now = FULL / norm(ref, s, mean, factor)
+        par[...] = jnp.concatenate(
+            [mean, factor, mine_now, jnp.zeros((5, rows), F32)], axis=0
+        )
+        turned = par[...].T
         colm[...] = jnp.broadcast_to(turned[:, 0:1], colm.shape)
         colf[...] = jnp.broadcast_to(turned[:, 1:2], colf.shape)
+        cole[...] = jnp.broadcast_to(turned[:, 2:3], cole.shape)
+        every = jnp.concatenate([norm(ref, t, mean, factor) for t in range(S)], axis=0)
+        turned_norms[:, 0:S] = every.T
 
     def scale(src, src_row, dst, dst_row, count, squares):
         def sixteen(i, _):
@@ -242,7 +281,7 @@
 
         lax.fori_loop(0, count // STEP, sixteen, 0)
 
-    columns(par)
+    columns(gat, mean, factor, tall)
     scale(code, 0, scaled, 0, rows, True)
 
     def rs_copy(owner, slot):
@@ -260,14 +299,26 @@
             left, scaled[...], (((1,), (1,)), ((), ())), preferred_element_type=F32
         )
 
+    level_row = level * (1.0 / FULL)
+
+    def hand_over(value, owner, row):
+        e = cole[pl.ds(pl.multiple_of(row, R), R), 0:1]
+
+        @pl.when(owner == s)
+        def _():
+            mine[...] = value
+
+        @pl.when(owner != s)
+        def _():
+            q = jnp.round(value * e * level_row)
+            q = jnp.clip(q, -32767.0, 32767.0)
+            part[owner] = q.astype(jnp.int32).astype(jnp.int16)
+            rs_copy(owner, s).start()
+
     def own_rows(k, _):
         owner = lax.rem(s + k, H)
         rows_here = pl.ds(pl.multiple_of(owner * R, R), R)
-        part[owner] = correlate(scaled[rows_here, :])
-
-        @pl.when(owner != s)
-        def _():
-            rs_copy(owner, s).start()
+        hand_over(correlate(scaled[rows_here, :]), owner, owner * R)
 
         return 0
 
@@ -302,7 +353,8 @@
     @pl.when(has_next)
     def _():
         par_copy.wait_recv()
-        columns(npar)
+        _, nmean, _, nfactor = moments(ngat)
+        columns(ngat, nmean, nfactor, ntall)
 
         def cross(k, _):
             c = lax.rem(k + s, NC)
@@ -311,11 +363,7 @@
             got = correlate(nscaled[...])
             for i in range(CH // R):
                 owner = H + c * (CH // R) + i
-                part[owner] = got[i * R : (i + 1) * R]
-
-                @pl.when(owner != s)
-                def _():
-                    rs_copy(owner, s).start()
+                hand_over(got[i * R : (i + 1) * R], owner, c * CH + i * R)
 
             return 0
 
@@ -334,17 +382,24 @@
 
     sent_to_me = jnp.logical_or(s < H, has_next)
 
-    @pl.when(sent_to_me)
+    def gather(norms, row):
+        ld_out[...] = mine[...]
+        for t in range(S):
+
+            @pl.when(t != s)
+            def _():
+                rs_copy(s, t).wait_recv()
+                col = norm(gat, t, mean, factor) * (1.0 / FULL)
+                e = norms[pl.ds(pl.multiple_of(row, R), R), t : t + 1]
+                ld_out[...] += rcv[t].astype(jnp.int32).astype(F32) * e * col
+
+    @pl.when(s < H)
     def _():
-        ld_out[...] = part[s]
-
-        def gather(d, _):
-            t = lax.rem(s + d, S)
-            rs_copy(s, t).wait_recv()
-            ld_out[...] += rcv[t]
-            return 0
-
-        lax.fori_loop(1, S, gather, 0)
+        gather(tall, s * R)
+
+    @pl.when(jnp.logical_and(s >= H, has_next))
+    def _():
+        gather(ntall, (s - H) * R)
 
     @pl.when(jnp.logical_not(sent_to_me))
     def _():
@@ -377,6 +432,19 @@
             return 0
 
         lax.fori_loop(0, NC, drain_codes, 0)
+
+
+def finish(stats, counts, ld, calls, share, mean, var, counts_o, ld_o, calls_o, share_o):
+    slabs = share.shape[0]
+    mean[...] = stats[0]
+    var[...] = stats[1]
+    counts_o[...] = counts[...]
+    ld_o[...] = ld[...]
+    for i in range(slabs):
+        here = slice(i * SLAB, (i + 1) * SLAB)
+        for q in range(2):
+            calls_o[q : q + 1, here] = calls[q * slabs + i : q * slabs + i + 1]
+        share_o[here] = share[i]
 
 
 def on_device(S, V, genotypes, weights):
@@ -404,16 +472,20 @@
             pltpu.VMEM((rows, width), BF16),
             pltpu.VMEM((rows, width), BF16),
             pltpu.VMEM((CH, width), BF16),
-            pltpu.VMEM((S, R, rows), F32),
-            pltpu.VMEM((S, R, rows), F32),
+            pltpu.VMEM((S, R, rows), jnp.int16),
+            pltpu.VMEM((R, rows), F32),
+            pltpu.VMEM((S, R, rows), jnp.int16),
             pltpu.VMEM((3, rows, LANES), F32),
             pltpu.VMEM((rows, LANES), jnp.int32),
             pltpu.VMEM((8, width), jnp.int32),
             pltpu.VMEM((8, width), F32),
             pltpu.VMEM((1, width), F32),
             pltpu.VMEM((S, 8, rows), F32),
+            pltpu.VMEM((S, 8, rows), F32),
             pltpu.VMEM((8, rows), F32),
-            pltpu.VMEM((8, rows), F32),
+            pltpu.VMEM((rows, LANES), F32),
+            pltpu.VMEM((rows, LANES), F32),
+            pltpu.VMEM((rows, LANES), F32),
             pltpu.VMEM((rows, LANES), F32),
             pltpu.VMEM((rows, LANES), F32),
             pltpu.VMEM((V, 3 * slabs, SLAB), F32),
@@ -434,14 +506,20 @@
         ),
         name="window_stats",
     )(genotypes, weights.reshape(1, width))
-    return (
-        stats[0],
-        stats[1],
-        counts,
-        ld,
-        calls.reshape(2, width),
-        share.reshape(width),
-    )
+    return pl.pallas_call(
+        finish,
+        out_shape=(
+            jax.ShapeDtypeStruct((rows,), F32),
+            jax.ShapeDtypeStruct((rows,), F32),
+            jax.ShapeDtypeStruct((4, rows), jnp.int32),
+            jax.ShapeDtypeStruct((R, rows), F32),
+            jax.ShapeDtypeStruct((2, width), jnp.int32),
+            jax.ShapeDtypeStruct((width,), F32),
+        ),
+        in_specs=[vmem] * 5,
+        out_specs=(vmem,) * 6,
+        name="finish",
+    )(stats, counts, ld, calls, share)
 
 
 def solution(mesh):

time: 89.2 us -> 74.2 us (0.83)
  Pallas kernels: 81.1 us -> 73.3 us
  local copies, waits for them, and re-layouts: 7.03 us -> 0 us
    pallas_call x1, Pallas kernels: 81.1 us -> 71.6 us  [on_device(): pl.pallas_call(functools.partial(kernel, S, V, CH), out_shape=(jax.ShapeD...]
    unnamed x3 -> x0, local copies, waits for them, and re-layouts: 4.29 us -> none
    pallas_call x0 -> x1, Pallas kernels: none -> 1.74 us  [on_device(): pl.pallas_call(finish, out_shape=(jax.ShapeDtypeStruct((rows,), F32), jax...]
    reshape x1 -> x0, local copies, waits for them, and re-layouts: 1.4 us -> none  [on_device(): calls.reshape(2, width)]
    slice x1 -> x0, local copies, waits for them, and re-layouts: 1.33 us -> none  [on_device(): stats[1]]
where the time goes in v2:
time: 74.2 us; the launch traced here: 73.9 us
  Pallas kernels  73.3 us (99%)
    pallas_call x1, Pallas kernels, on_device(): pl.pallas_call(functools.partial(kernel, S, V, CH), out_shape=(jax.ShapeD...  71.6 us
    pallas_call x1, Pallas kernels, on_device(): pl.pallas_call(finish, out_shape=(jax.ShapeDtypeStruct((rows,), F32), jax...  1.74 us

profile of v2, /device:TPU:21, one launch (start us, length us, event | category | flops | bytes accessed | tf_op | source)
XLA Modules:
  0.0 73.9 jit_solution(16150237757611118358)
XLA Ops:
  0.6 71.6 %window_stats.1 = (f32[2,512]{1,0:T(2,128)}, s32[4,512]{1,0:T(4,128)}, f32[128,512]{1,0:T(8,128)}, s32[16,512]{1,0:T(8,128)}, f32[8,512]{1,0:T(8,128)}) custom-call(s32[512,4096]{1,0:T(8,128)} %gen_hbm.1, f32[1,4096]{1,0:T(1,128)} %bitcast.1), custom_call_target="tpu_custom_call" | custom-call | tf_op jit(solution)/shard_map/window_stats/pallas_call | solution.py:458
  72.2 1.7 %finish.1 = (f32[512]{0:T(512)}, f32[512]{0:T(512)}, s32[4,512]{1,0:T(4,128)}, f32[128,512]{1,0:T(8,128)}, s32[2,4096]{1,0:T(2,128)}, /*index=5*/f32[4096]{0:T(1024)}) custom-call(f32[2,512]{1,0:T(2,128)} %get-tuple-element.11.stats, s32[4,512]{1,0:T(4,128)} %get-tuple-element.12.counts, f32[128,512]{1,0:T(8,128)} %get-tuple-element.13.ld, ...), custom_call_target="tpu_custom_call" | custom-call | tf_op jit(solution)/shard_map/finish/pallas_call | solution.py:509
